TPU v7x, 256 devices: a whole 4x4x8 slice. The times are simulated.
256 devices in a mesh: seq: 16 (over z, core), grp: 2 (over y_hi), dp: 8 (over y_lo, x).
Axes of the slice: x: 4, y: 4 (y_hi: 2, y_lo: 2; y = y_hi * 2 + y_lo), z: 8, core: 2. Of those that a mesh axis runs over, the one named last changes fastest.
Arguments:
- clips: bfloat16 [8, 2048, 1408], P('dp', 'seq'), may hold values from -6 to 6
- context: int32 [8, 2048], P('dp', 'seq'), may hold values from 0 to 1, as said below
- predict_index: int32 [8, 3072], P('dp', 'seq'), may hold values from -1 to 2047, as said below
- target_qkv: bfloat16 [3, 1408, 1408], P(None, 'dp', 'grp'), may hold values from -8 to 8
- target_out: bfloat16 [1408, 1408], P('grp'), may hold values from -0.15625 to 0.15625
- student_qkv: bfloat16 [3, 1408, 1408], P(None, 'dp', 'grp'), may hold values from -8 to 8
- student_out: bfloat16 [1408, 1408], P('grp', 'dp'), may hold values from -0.15625 to 0.15625
- mask_token: float32 [1408], replicated, may hold values from -4 to 4
Outputs:
- out_grad: float32 [1408, 1408], P('grp', 'dp')
- target_blend: float32 [1408, 1408], P('grp')
Inputs may be any that keep to these rules, and one draw needn't show every extreme that they name: In every aligned block of 128 tokens of a clip exactly 32 tokens have context 1 and the others 0. `predict_index`: each device's 192 slots name distinct target positions (context 0) of its clip, followed by -1 in the unused slots; different devices' lists may name the same position. In every clip one list is full.
All inputs are finite; a program needn't handle non-finite values.
Results may differ from a plain program's by a relative error of at most 0.014.
Values may be sent and summed in bfloat16 or wider, within the bound.
No kernel may reach another device: no remote copies, remote signals or barrier semaphores. Data moves between devices by JAX's collectives and lax.ppermute only.
A program may use at most 128 MiB of HBM per device.

v0:
```python
import math
import jax
import jax.numpy as jnp
from jax import lax
from jax.sharding import PartitionSpec as P

HEAD_DIM = 88
CTX_DEV = 32
EPSILON = 1e-06
MOMENTUM = 0.99


def side_by_side(arrays, axis, dim, along):
    ends, at = ([], 0)
    for a in arrays[:-1]:
        at += a.shape[along]
        ends.append(at)
    both = jnp.concatenate(arrays, axis=along)
    return tuple(jnp.split(lax.all_gather(both, axis, axis=dim, tiled=True), ends, axis=along))


def from_everyone(shard, axis):
    copies = jnp.broadcast_to(shard, (lax.axis_size(axis), *shard.shape))
    return lax.all_to_all(copies, axis, split_axis=0, concat_axis=0, tiled=True)


def taken_together(shard, axis):
    return from_everyone(shard, axis).astype(jnp.float32).sum(axis=0)


def in_order(tiles, dim):
    shape = list(tiles.shape[1:])
    shape[dim] *= tiles.shape[0]
    return jnp.moveaxis(tiles, 0, dim).reshape(shape)


def collect(shard, axis, dim):
    return in_order(from_everyone(shard, axis), dim)


def total_of_pieces(shard, axis):
    return lax.all_gather(shard, axis).astype(jnp.float32).sum(0)


def layer_norm(values):
    center = values - jnp.mean(values, axis=-1, keepdims=True)
    factor = lax.rsqrt(jnp.mean(center * center, axis=-1, keepdims=True) + EPSILON)
    return (center * factor, factor)


def position_table(places, width):
    half_width = width // 2
    spacing = jnp.exp(jnp.arange(half_width, dtype=jnp.float32) * (-math.log(10000.0) / half_width))
    angles = places.astype(jnp.float32)[:, None] * spacing[None, :]
    return jnp.concatenate([jnp.sin(angles), jnp.cos(angles)], axis=1)


def to_heads(queries):
    head_count = queries.shape[1] // HEAD_DIM
    return queries.reshape(queries.shape[0], head_count, HEAD_DIM).transpose(1, 0, 2)


def empty_state(head_count, row_count):
    peaks = jnp.full((head_count, row_count), -1e30, jnp.float32)
    totals = jnp.zeros((head_count, row_count), jnp.float32)
    summed = jnp.zeros((head_count, row_count, HEAD_DIM), jnp.float32)
    return (peaks, totals, summed)


def from_heads(running):
    peaks, totals, summed = running
    mixed = summed / totals[:, :, None]
    head_count, row_count, unused = mixed.shape
    return mixed.transpose(1, 0, 2).reshape(row_count, head_count * HEAD_DIM).astype(jnp.bfloat16)


def attend_shard(running, shard_rows, query_heads):
    peaks, totals, summed = running
    key_rows, value_rows = shard_rows
    length = key_rows.shape[0]
    head_count = query_heads.shape[0]
    key_heads = key_rows.reshape(length, head_count, HEAD_DIM)
    value_heads = value_rows.reshape(length, head_count, HEAD_DIM)
    factor = HEAD_DIM ** (-0.5)
    scores = (
        jnp.einsum("hqd,khd->hqk", query_heads, key_heads, preferred_element_type=jnp.float32)
        * factor
    )
    raised = jnp.maximum(peaks, jnp.max(scores, axis=2))
    shifted = jnp.exp(scores - raised[:, :, None])
    totals = jnp.sum(shifted, axis=2)
    summed = jnp.einsum(
        "hqk,khd->hqd",
        shifted.astype(jnp.bfloat16),
        value_heads,
        preferred_element_type=jnp.float32,
    )
    return (raised, totals, summed)


def body(
    clips, context, predict_index, target_qkv, target_out, student_qkv, student_out, mask_token
):
    tokens = clips[0]
    keep_flags = context[0]
    listed = predict_index[0]
    row_count, width = tokens.shape
    half_width = target_qkv.shape[2]
    head_count = half_width // HEAD_DIM
    normed = layer_norm(tokens.astype(jnp.float32))[0].astype(jnp.bfloat16)
    projected = jnp.einsum(
        "nr,krc->knc",
        normed,
        lax.all_gather(target_qkv, "dp", axis=1, tiled=True),
        preferred_element_type=jnp.float32,
    )
    projected = projected.astype(jnp.bfloat16)
    target_state = attend_shard(
        empty_state(head_count, row_count),
        side_by_side((projected[1], projected[2]), "seq", 0, 1),
        query_heads=to_heads(projected[0]),
    )
    target_mixed = from_heads(target_state)
    target_part = jnp.dot(target_mixed, target_out, preferred_element_type=jnp.float32)
    target_sum = taken_together(target_part.astype(jnp.bfloat16), "grp").astype(jnp.float32)
    features = layer_norm(tokens.astype(jnp.float32) + target_sum)[0].astype(jnp.bfloat16)
    first_row = lax.axis_index("seq") * row_count
    every_list = lax.all_gather(listed, "seq", axis=0, tiled=True)
    places = first_row + jnp.arange(row_count, dtype=jnp.int32)
    usable = jnp.sum((every_list[None, :] == places[:, None]).astype(jnp.float32), axis=1)
    slot_count = places.shape[0]
    is_context = keep_flags == 1
    context_order = jnp.cumsum(is_context.astype(jnp.int32)) - 1
    selector = (
        (context_order[None, :] == jnp.arange(CTX_DEV, dtype=jnp.int32)[:, None])
        & is_context[None, :]
    ).astype(jnp.bfloat16)
    context_rows = jnp.dot(selector, normed, preferred_element_type=jnp.float32).astype(
        jnp.bfloat16
    )
    seeds = mask_token[None, :] + position_table(jnp.maximum(places, 0), width)
    seed_normed = layer_norm(seeds)[0].astype(jnp.bfloat16)
    shard_rows = lax.all_gather(student_qkv, "dp", axis=1, tiled=True)
    query_total = jnp.dot(seed_normed, shard_rows[0], preferred_element_type=jnp.float32)
    pair_total = jnp.einsum(
        "nr,krc->knc", context_rows, shard_rows[1:], preferred_element_type=jnp.float32
    )
    student_pairs = pair_total
    student_pairs = student_pairs.astype(jnp.bfloat16)
    student_state = attend_shard(
        empty_state(head_count, slot_count),
        side_by_side((student_pairs[0], student_pairs[1]), "seq", 0, 1),
        query_heads=to_heads(query_total.astype(jnp.bfloat16)),
    )
    student_mixed = from_heads(student_state)
    relaid = collect(student_out, "dp", 1)
    student_part = jnp.dot(student_mixed, relaid, preferred_element_type=jnp.float32)
    student_sum = taken_together(student_part.astype(jnp.bfloat16), "grp").astype(jnp.float32)
    predicted, factor = layer_norm(seeds + student_sum)
    wanted = features.astype(jnp.float32)
    slope = jnp.clip(predicted - wanted, -1.0, 1.0) * usable[:, None]
    back_grad = (
        slope
        - jnp.mean(slope, axis=1, keepdims=True)
        - predicted * jnp.mean(slope * predicted, axis=1, keepdims=True)
    ) * factor
    arrived_grad = lax.all_to_all(
        back_grad.astype(jnp.bfloat16), "dp", split_axis=1, concat_axis=0, tiled=True
    ).astype(back_grad.dtype)
    column_grad = jnp.dot(
        collect(student_mixed, "dp", 0).astype(jnp.float32).T,
        arrived_grad,
        precision=lax.Precision.HIGHEST,
    )
    out_grad = total_of_pieces(column_grad.astype(jnp.bfloat16), "seq").astype(jnp.float32)
    target_blend = MOMENTUM * target_out.astype(jnp.float32) + (1.0 - MOMENTUM) * relaid.astype(
        jnp.float32
    )
    return (out_grad, target_blend)


def solution(mesh):
    in_specs = (
        P("dp", "seq", None),
        P("dp", "seq"),
        P("dp", "seq"),
        P(None, "dp", "grp"),
        P("grp", None),
        P(None, "dp", "grp"),
        P("grp", "dp"),
        P(),
    )
    out_specs = (P("grp", "dp"), P("grp", None))
    return jax.shard_map(body, mesh=mesh, in_specs=in_specs, out_specs=out_specs, check_vma=False)
```

profile of v0, /device:TPU:1, one launch (start us, length us, event | category | flops | bytes accessed | tf_op | source)
XLA Modules:
  0.0 378.8 jit_solution(2084272642977128158)
XLA Ops:
  9.7 1.1 convert_reduce_fusion.4
  10.9 1.2 multiply_reduce_fusion.5
  12.1 77.9 %all-gather.9.cloned.1.call-done = bf16[3,1408,704]{2,1,0:T(8,128)(2,1)} async-done(((bf16[3,176,704]{2,1,0:T(8,128)(2,1)}), bf16[3,1408,704]{2,1,0:T(8,128)(2,1)}) %all-gather.9.cloned.1.call-update) | async-done | bytes 5947408 | tf_op jit(solution)/shard_map/all_gather | solution.py:143
  90.0 3.4 fusion.24
  93.4 0.7 pad_maximum_fusion.1
  94.2 73.0 %all-gather.13.cloned.1.call-done = bf16[3,1408,704]{2,1,0:T(8,128)(2,1)} async-done(((bf16[3,176,704]{2,1,0:T(8,128)(2,1)}), bf16[3,1408,704]{2,1,0:T(8,128)(2,1)}) %all-gather.13.cloned.1.call-update) | async-done | bytes 5947408 | tf_op jit(solution)/shard_map/all_gather | solution.py:114
  167.2 5.4 %fusion.12 = bf16[3,128,704]{1,2,0:T(8,128)(2,1)S(1)} fusion(bf16[3,1408,704]{2,1,0:T(8,128)(2,1)} %all-gather.13.cloned.1.call-done, bf16[1,128,1408]{2,1,0:T(8,128)(2,1)S(1)} %copy-done, f32[128]{0:T(128)S(1)} %add_rsqrt_fusion.2, f32[128]{0:T(128)S(1)} %broadcast_multiply_fusion.4), kind=kOutput, calls=%fused_computation.25 | convolution fusion | flops 762257408 | bytes 6849536 | tf_op jit(solution)/shard_map/nr,krc->knc/dot_general | solution.py:111
  172.5 0.7 fusion.62
  173.2 0.8 pad_maximum_fusion
  174.1 1.5 broadcast_in_dim.9
  175.5 3.7 all-to-all-start.1
  179.3 1.4 multiply_sine_fusion
  183.0 46.7 %all-reduce = s32[3072]{0:T(1024)S(1)} all-reduce(s32[3072]{0:T(1024)S(1)} %dynamic-update-slice), channel_id=2, replica_groups=mesh['seq'=16,'grp'=2,'dp'=8] {'seq'}, use_global_device_ids=true, to_apply=%add | all-reduce | flops 3072 | bytes 24576
  229.7 2.7 fusion.18
  232.4 3.0 fusion.61
  235.5 1.4 copy.38
  236.9 2.3 copy.39
  241.1 0.8 convolution_convert_fusion.1
  241.9 0.9 broadcast_in_dim.10
  242.8 4.5 %all-to-all-start.2 = ((bf16[2,128,1408]{2,1,0:T(8,128)(2,1)}), bf16[2,128,1408]{2,1,0:T(8,128)(2,1)}, u32[]{:S(2)}, u32[]{:S(2)}) async-start(bf16[2,128,1408]{2,1,0:T(8,128)(2,1)} %broadcast_in_dim.10), calls=%async_computation.2 | async-start | bytes 1441792 | tf_op jit(solution)/shard_map/all_to_all | solution.py:24
  247.6 1.0 copy.41
  248.8 2.2 multiply_sine_fusion.1
  251.0 4.2 %all-to-all-done.2 = bf16[2,128,1408]{2,1,0:T(8,128)(2,1)} async-done(((bf16[2,128,1408]{2,1,0:T(8,128)(2,1)}), bf16[2,128,1408]{2,1,0:T(8,128)(2,1)}, u32[]{:S(2)}, u32[]{:S(2)}) %all-to-all-start.2) | async-done | bytes 720928 | tf_op jit(solution)/shard_map/all_to_all | solution.py:24
  255.2 1.3 convert_reduce_fusion.3
  256.5 0.8 copy-done.3
  257.4 1.2 copy.40
  258.6 1.6 fusion.58
  260.2 2.5 all-gather.15.cloned.1.call-done
  262.7 3.2 fusion.60
  265.9 1.4 multiply_reduce_fusion
  267.3 1.6 fusion
  269.0 1.7 fusion.33
  271.2 0.9 broadcast_in_dim.11
  272.2 4.3 %all-to-all-start.3 = ((bf16[2,128,1408]{2,1,0:T(8,128)(2,1)}), bf16[2,128,1408]{2,1,0:T(8,128)(2,1)}, u32[]{:S(2)}, u32[]{:S(2)}) async-start(bf16[2,128,1408]{2,1,0:T(8,128)(2,1)} %broadcast_in_dim.11), calls=%async_computation.3 | async-start | bytes 1441792 | tf_op jit(solution)/shard_map/all_to_all | solution.py:24
  276.7 8.6 %all-to-all-done.3 = bf16[2,128,1408]{2,1,0:T(8,128)(2,1)} async-done(((bf16[2,128,1408]{2,1,0:T(8,128)(2,1)}), bf16[2,128,1408]{2,1,0:T(8,128)(2,1)}, u32[]{:S(2)}, u32[]{:S(2)}) %all-to-all-start.3) | async-done | bytes 720928 | tf_op jit(solution)/shard_map/all_to_all | solution.py:24
  285.3 1.3 broadcast_in_dim.8
  286.6 4.3 %all-to-all-start = ((bf16[8,128,704]{1,2,0:T(8,128)(2,1)}), bf16[8,128,704]{1,2,0:T(8,128)(2,1)}, u32[]{:S(2)}, u32[]{:S(2)}) async-start(bf16[8,128,704]{1,2,0:T(8,128)(2,1)} %broadcast_in_dim.8), calls=%async_computation | async-start | bytes 2883584 | tf_op jit(solution)/shard_map/all_to_all | solution.py:24
  291.0 1.3 convert_reduce_fusion.2
  292.4 1.1 copy.42
  293.8 1.7 fusion.39
  296.0 14.9 %all-to-all-done = bf16[8,128,704]{1,2,0:T(8,128)(2,1)} async-done(((bf16[8,128,704]{1,2,0:T(8,128)(2,1)}), bf16[8,128,704]{1,2,0:T(8,128)(2,1)}, u32[]{:S(2)}, u32[]{:S(2)}) %all-to-all-start) | async-done | bytes 1441824 | tf_op jit(solution)/shard_map/all_to_all | solution.py:24
  310.9 9.1 %all_to_all.33 = bf16[128,8,176]{0,2,1:T(8,128)(2,1)S(1)} all-to-all(bf16[128,8,176]{0,2,1:T(8,128)(2,1)S(1)} %multiply_convert_fusion), channel_id=1, replica_groups=mesh['seq'=16,'grp'=2,'dp'=8] {'dp'}, dimensions={1} | all-to-all | bytes 720896 | tf_op jit(solution)/shard_map/all_to_all | solution.py:167
  320.0 2.7 fusion.20
  322.7 4.0 %copy.43 = bf16[704,1408]{0,1:T(8,128)(2,1)} copy(bf16[704,1408]{1,0:T(8,128)(2,1)} %param.12) | data formatting | bytes 3964928 | tf_op args[4]
  326.6 4.4 %multiply_add_fusion = f32[704,1408]{0,1:T(8,128)} fusion(bf16[704,1408]{0,1:T(8,128)(2,1)} %copy.43, bf16[8,704,176]{1,2,0:T(8,128)(2,1)S(1)} %all-to-all-done.1), kind=kLoop, calls=%fused_computation.7 | loop fusion | flops 4956160 | bytes 7929856 | tf_op jit(solution)/shard_map/add | solution.py:176
  331.0 5.6 %copy.44 = f32[704,1408]{1,0:T(8,128)} copy(f32[704,1408]{0,1:T(8,128)} %multiply_add_fusion) | data formatting | bytes 7929856
  336.6 31.9 %all-gather.17.cloned.1.call-done = bf16[16,704,176]{1,2,0:T(8,128)(2,1)} async-done(((bf16[1,704,176]{1,2,0:T(8,128)(2,1)}), bf16[16,704,176]{1,2,0:T(8,128)(2,1)}) %all-gather.17.cloned.1.call-update) | async-done | bytes 3964944 | tf_op jit(solution)/shard_map/all_gather | solution.py:42
  368.5 3.8 convert_reduce_fusion
  (80 shorter events, 8.1 us)
Async XLA Ops:
  7.2 82.8 %all-gather.9.cloned.1.call-start = ((), (), s32[]{:S(2)}) async-start(), calls=%async_computation.5 | async-start | bytes 7299072 | tf_op jit(solution)/shard_map/all_gather | solution.py:143
  7.9 159.3 %all-gather.13.cloned.1.call-start = ((), (), s32[]{:S(2)}) async-start(), calls=%async_computation.7 | async-start | bytes 7299072 | tf_op jit(solution)/shard_map/all_gather | solution.py:114
  8.6 223.8 %all-gather.11.cloned.1.call-start = ((), (), s32[]{:S(2)}) async-start(), calls=%async_computation.6 | async-start | bytes 1531904 | tf_op jit(solution)/shard_map/all_gather | solution.py:19
  12.1 155.1 %copy-start = (bf16[1,128,1408]{2,1,0:T(8,128)(2,1)S(1)}, bf16[1,128,1408]{2,1,0:T(8,128)(2,1)}, u32[]{:S(2)}) copy-start(bf16[1,128,1408]{2,1,0:T(8,128)(2,1)} %param.8) | copy-start | bytes 1081348
  94.1 79.9 %copy-start.13 = (bf16[704,176]{0,1:T(8,128)(2,1)S(1)}, bf16[704,176]{0,1:T(8,128)(2,1)}, u32[]{:S(2)}) copy-start(bf16[704,176]{0,1:T(8,128)(2,1)} %param.14) | copy-start | bytes 743428
  94.1 168.5 %all-gather.15.cloned.1.call-start = ((), (), s32[]{:S(2)}) async-start(), calls=%async_computation.8 | async-start | bytes 6127616 | tf_op jit(solution)/shard_map/all_gather | solution.py:19
  175.5 5.3 %copy-start.14 = (f32[1408]{0:T(1024)S(1)}, f32[1408]{0:T(1024)}, u32[]{:S(2)}) copy-start(f32[1408]{0:T(1024)} %param.15) | copy-start | bytes 16900
  175.5 5.8 %copy-start.16 = (u32[256]{0:T(256)S(1)}, u32[256]{0:T(256)}, u32[]{:S(2)}) copy-start(u32[256]{0:T(256)} %constant.56) | copy-start | bytes 3076
  175.5 7.2 %copy-start.15 = (s32[1,192]{1,0:T(1,128)S(1)}, s32[1,192]{1,0:T(1,128)}, u32[]{:S(2)}) copy-start(s32[1,192]{1,0:T(1,128)} %param.10) | copy-start | bytes 2308
  175.5 65.5 %all-to-all-start.1 = ((bf16[8,704,176]{1,2,0:T(8,128)(2,1)}), bf16[8,704,176]{1,2,0:T(8,128)(2,1)S(1)}, u32[]{:S(2)}, u32[]{:S(2)}) async-start(bf16[8,704,176]{1,2,0:T(8,128)(2,1)} %broadcast_in_dim.9), calls=%async_computation.1 | async-start | bytes 4325376 | tf_op jit(solution)/shard_map/all_to_all | solution.py:24
  180.8 54.7 %copy-start.4 = (f32[128,704]{1,0:T(8,128)}, f32[128,704]{1,0:T(8,128)S(1)}, u32[]{:S(2)}) copy-start(f32[128,704]{1,0:T(8,128)S(1)} %get-tuple-element.23) | copy-start | bytes 1081348
  180.8 54.7 %copy-start.5 = (f32[128,704]{1,0:T(8,128)}, f32[128,704]{1,0:T(8,128)S(1)}, u32[]{:S(2)}) copy-start(f32[128,704]{1,0:T(8,128)S(1)} %get-tuple-element.24) | copy-start | bytes 1081348
  239.2 1.2 copy-start.11
  242.8 12.4 %all-to-all-start.2 = ((bf16[2,128,1408]{2,1,0:T(8,128)(2,1)}), bf16[2,128,1408]{2,1,0:T(8,128)(2,1)}, u32[]{:S(2)}, u32[]{:S(2)}) async-start(bf16[2,128,1408]{2,1,0:T(8,128)(2,1)} %broadcast_in_dim.10), calls=%async_computation.2 | async-start | bytes 1441792 | tf_op jit(solution)/shard_map/all_to_all | solution.py:24
  256.5 0.9 copy-start.3
  260.2 16.3 %copy-start.2 = (f32[128,1408]{1,0:T(8,128)}, f32[128,1408]{1,0:T(8,128)S(1)}, u32[]{:S(2)}) copy-start(f32[128,1408]{1,0:T(8,128)S(1)} %get-tuple-element.11) | copy-start | bytes 2162692
  262.7 3.2 copy-start.12
  269.0 1.8 copy-start.1
  272.2 13.2 %all-to-all-start.3 = ((bf16[2,128,1408]{2,1,0:T(8,128)(2,1)}), bf16[2,128,1408]{2,1,0:T(8,128)(2,1)}, u32[]{:S(2)}, u32[]{:S(2)}) async-start(bf16[2,128,1408]{2,1,0:T(8,128)(2,1)} %broadcast_in_dim.11), calls=%async_computation.3 | async-start | bytes 1441792 | tf_op jit(solution)/shard_map/all_to_all | solution.py:24
  286.6 24.2 %all-to-all-start = ((bf16[8,128,704]{1,2,0:T(8,128)(2,1)}), bf16[8,128,704]{1,2,0:T(8,128)(2,1)}, u32[]{:S(2)}, u32[]{:S(2)}) async-start(bf16[8,128,704]{1,2,0:T(8,128)(2,1)} %broadcast_in_dim.8), calls=%async_computation | async-start | bytes 2883584 | tf_op jit(solution)/shard_map/all_to_all | solution.py:24
  290.9 77.6 %all-gather.17.cloned.1.call-start = ((), (), s32[]{:S(2)}) async-start(), calls=%async_computation.9 | async-start | bytes 4595712 | tf_op jit(solution)/shard_map/all_gather | solution.py:42
  293.6 2.0 copy-start.6
  293.6 2.0 copy-start.7
  293.6 2.0 copy-start.8
  293.6 2.0 copy-start.9
  293.6 2.0 copy-start.10
Sparse Core Ops, SparseCore 0:
  9.8 80.1 all-gather.8
  91.8 75.3 all-gather.12
  169.0 38.1 all-gather.10
  208.8 53.8 all-gather.14
  322.8 45.6 all-gather.16
where the time goes:
time: 380 us; the launch traced here: 379 us
  waiting for transfers between devices  214 us (56%)
  blocking collectives  55.8 us (15%)
  local copies, waits for them, and re-layouts  30.3 us (8%)
  other arithmetic  26.6 us (7%)
  matrix products  19.8 us (5%)
  starting transfers between devices  17 us (4%)
  between operations  14.9 us (4%)
    all_gather x1, waiting for transfers between devices, body(): shard_rows = lax.all_gather(student_qkv, 'dp', axis=1, tiled=True)  77.9 us
    all_gather x1, waiting for transfers between devices, body(): lax.all_gather(target_qkv, 'dp', axis=1, tiled=True)  73 us
    unnamed x1, blocking collectives  46.7 us
    all_gather x1, waiting for transfers between devices, total_of_pieces(): return lax.all_gather(shard, axis).astype(jnp.float32).sum(0)  31.9 us
    all_to_all x4, waiting for transfers between devices, from_everyone(): return lax.all_to_all(copies, axis, split_axis=0, concat_axis=0, tiled=True)  27.7 us
    all_to_all x4, starting transfers between devices, from_everyone(): return lax.all_to_all(copies, axis, split_axis=0, concat_axis=0, tiled=True)  16.8 us
    unnamed x39, local copies, waits for them, and re-layouts  11.5 us
    split x4, local copies, waits for them, and re-layouts, side_by_side(): jnp.split(lax.all_gather(both, axis, axis=dim, tiled=True), ends, axis=al...  9.96 us
  transfers between devices with their start and end apart: 9, of which 7 were waited for; matrix products, arithmetic and copies ran while one was open for 15% of the time, Pallas kernels for 0%

commit v1 on v0

--- a/solution.py
+++ b/solution.py
@@ -101,6 +101,18 @@
 def body(
     clips, context, predict_index, target_qkv, target_out, student_qkv, student_out, mask_token
 ):
+
+    def press_case_for(x0, join_dim):
+        return jnp.concatenate(
+            jax.lax.all_to_all(
+                jnp.stack([x0] * jax.lax.axis_size("dp")),
+                split_axis=0,
+                axis_name="dp",
+                concat_axis=0,
+            ),
+            axis=join_dim,
+        )
+
     tokens = clips[0]
     keep_flags = context[0]
     listed = predict_index[0]
@@ -109,10 +121,7 @@
     head_count = half_width // HEAD_DIM
     normed = layer_norm(tokens.astype(jnp.float32))[0].astype(jnp.bfloat16)
     projected = jnp.einsum(
-        "nr,krc->knc",
-        normed,
-        lax.all_gather(target_qkv, "dp", axis=1, tiled=True),
-        preferred_element_type=jnp.float32,
+        "nr,krc->knc", normed, press_case_for(target_qkv, 1), preferred_element_type=jnp.float32
     )
     projected = projected.astype(jnp.bfloat16)
     target_state = attend_shard(

time: 380 us -> 399 us (1.050)
  starting transfers between devices: 17 us -> 25.9 us
  blocking collectives: 55.8 us -> 63.4 us
  local copies, waits for them, and re-layouts: 30.3 us -> 37.9 us
    all_gather x1, waiting for transfers between devices: 77.9 us -> 156 us  [body(): shard_rows = lax.all_gather(student_qkv, 'dp', axis=1, tiled=True)]
    all_gather x1 -> x0, waiting for transfers between devices: 73 us -> none  [body(): lax.all_gather(target_qkv, 'dp', axis=1, tiled=True)]
    unnamed x1, blocking collectives: 46.7 us -> 52.8 us
    all_to_all x0 -> x1, starting transfers between devices: none -> 5.98 us  [press_case_for(): jax.lax.all_to_all(jnp.stack([x0] * jax.lax.axis_size('dp')), split_axis=...]
    another operation x1 -> x2, local copies, waits for them, and re-layouts: 0.11 us -> 4.33 us  [the longest x1 4.21 us: press_case_for(): jnp.stack([x0] * jax.lax.axis_size('dp'))]
    unnamed x39 -> x41, local copies, waits for them, and re-layouts: 11.5 us -> 11.4 us
  transfers between devices with their start and end apart: 9 -> 9, of which waited for: 7 -> 5; matrix products, arithmetic and copies ran while one was open for 15% -> 15% of each run, Pallas kernels for 0% -> 0%
where the time goes in v1:
time: 399 us; the launch traced here: 398 us
  waiting for transfers between devices  215 us (54%)
  blocking collectives  63.4 us (16%)
  local copies, waits for them, and re-layouts  37.9 us (9%)
  starting transfers between devices  25.9 us (6%)
  other arithmetic  23.9 us (6%)
  matrix products  17 us (4%)
  between operations  14.8 us (4%)
    all_gather x1, waiting for transfers between devices, body(): shard_rows = lax.all_gather(student_qkv, 'dp', axis=1, tiled=True)  156 us
    unnamed x1, blocking collectives  52.8 us
    all_gather x1, waiting for transfers between devices, total_of_pieces(): return lax.all_gather(shard, axis).astype(jnp.float32).sum(0)  33.4 us
    all_to_all x4, waiting for transfers between devices, from_everyone(): return lax.all_to_all(copies, axis, split_axis=0, concat_axis=0, tiled=True)  25 us
    all_to_all x4, starting transfers between devices, from_everyone(): return lax.all_to_all(copies, axis, split_axis=0, concat_axis=0, tiled=True)  19.5 us
    unnamed x41, local copies, waits for them, and re-layouts  11.4 us
    all_to_all x1, blocking collectives, body(): lax.all_to_all(back_grad.astype(jnp.bfloat16), 'dp', split_axis=1, concat...  10.6 us
    split x4, local copies, waits for them, and re-layouts, side_by_side(): jnp.split(lax.all_gather(both, axis, axis=dim, tiled=True), ends, axis=al...  10.1 us
  transfers between devices with their start and end apart: 9, of which 5 were waited for; matrix products, arithmetic and copies ran while one was open for 15% of the time, Pallas kernels for 0%

profile of v1, /device:TPU:1, one launch (start us, length us, event | category | flops | bytes accessed | tf_op | source)
XLA Modules:
  0.0 397.8 jit_solution(11555283631176557462)
XLA Ops:
  7.9 4.2 %stack.2 = bf16[8,3,176,704]{3,2,1,0:T(8,128)(2,1)} broadcast(bf16[3,176,704]{2,1,0:T(8,128)(2,1)} %param.11), dimensions={1,2,3} | broadcast | bytes 6690816 | tf_op jit(solution)/shard_map/stack | solution.py:108
  12.1 6.0 %all-to-all-start.3 = ((bf16[8,3,176,704]{3,2,1,0:T(8,128)(2,1)}), bf16[8,3,176,704]{3,2,1,0:T(8,128)(2,1)}, u32[]{:S(2)}, u32[]{:S(2)}) async-start(bf16[8,3,176,704]{3,2,1,0:T(8,128)(2,1)} %stack.2), calls=%async_computation.3 | async-start | bytes 12976128 | tf_op jit(solution)/shard_map/all_to_all | solution.py:107
  19.0 155.7 %all-gather.8.cloned.1.call-done = bf16[3,1408,704]{2,1,0:T(8,128)(2,1)} async-done(((bf16[3,176,704]{2,1,0:T(8,128)(2,1)}), bf16[3,1408,704]{2,1,0:T(8,128)(2,1)}) %all-gather.8.cloned.1.call-update) | async-done | bytes 5947408 | tf_op jit(solution)/shard_map/all_gather | solution.py:152
  174.7 3.3 fusion.24
  178.0 0.7 pad_maximum_fusion.1
  178.8 3.3 copy.46
  182.1 2.6 fusion.12
  184.7 0.7 fusion.69
  185.4 0.8 pad_maximum_fusion
  186.2 1.5 broadcast_in_dim.9
  187.7 6.1 %all-to-all-start.1 = ((bf16[8,704,176]{1,2,0:T(8,128)(2,1)}), bf16[8,704,176]{1,2,0:T(8,128)(2,1)S(1)}, u32[]{:S(2)}, u32[]{:S(2)}) async-start(bf16[8,704,176]{1,2,0:T(8,128)(2,1)} %broadcast_in_dim.9), calls=%async_computation.1 | async-start | bytes 4325376 | tf_op jit(solution)/shard_map/all_to_all | solution.py:24
  193.8 1.4 multiply_sine_fusion
  197.4 52.8 %all-reduce = s32[3072]{0:T(1024)S(1)} all-reduce(s32[3072]{0:T(1024)S(1)} %dynamic-update-slice), channel_id=2, replica_groups=mesh['seq'=16,'grp'=2,'dp'=8] {'seq'}, use_global_device_ids=true, to_apply=%add | all-reduce | flops 3072 | bytes 24576
  250.2 2.7 fusion.18
  253.0 3.0 fusion.68
  256.0 1.4 copy.42
  257.4 2.3 copy.43
  260.8 0.7 fusion.19
  261.5 0.8 convolution_convert_fusion.1
  262.4 0.9 broadcast_in_dim.10
  263.3 4.3 %all-to-all-start.2 = ((bf16[2,128,1408]{2,1,0:T(8,128)(2,1)}), bf16[2,128,1408]{2,1,0:T(8,128)(2,1)}, u32[]{:S(2)}, u32[]{:S(2)}) async-start(bf16[2,128,1408]{2,1,0:T(8,128)(2,1)} %broadcast_in_dim.10), calls=%async_computation.2 | async-start | bytes 1441792 | tf_op jit(solution)/shard_map/all_to_all | solution.py:24
  267.9 1.1 copy.45
  269.0 2.2 multiply_sine_fusion.1
  271.2 4.4 %all-to-all-done.2 = bf16[2,128,1408]{2,1,0:T(8,128)(2,1)} async-done(((bf16[2,128,1408]{2,1,0:T(8,128)(2,1)}), bf16[2,128,1408]{2,1,0:T(8,128)(2,1)}, u32[]{:S(2)}, u32[]{:S(2)}) %all-to-all-start.2) | async-done | bytes 720928 | tf_op jit(solution)/shard_map/all_to_all | solution.py:24
  275.6 1.3 convert_reduce_fusion.3
  276.9 0.8 copy-done.3
  277.8 1.1 copy.44
  278.9 1.6 fusion.65
  280.6 3.4 fusion.67
  284.0 1.4 multiply_reduce_fusion
  285.4 1.6 fusion
  287.1 1.7 fusion.33
  289.4 0.9 broadcast_in_dim.11
  290.3 4.3 %all-to-all-start.4 = ((bf16[2,128,1408]{2,1,0:T(8,128)(2,1)}), bf16[2,128,1408]{2,1,0:T(8,128)(2,1)}, u32[]{:S(2)}, u32[]{:S(2)}) async-start(bf16[2,128,1408]{2,1,0:T(8,128)(2,1)} %broadcast_in_dim.11), calls=%async_computation.4 | async-start | bytes 1441792 | tf_op jit(solution)/shard_map/all_to_all | solution.py:24
  294.8 7.8 %all-to-all-done.4 = bf16[2,128,1408]{2,1,0:T(8,128)(2,1)} async-done(((bf16[2,128,1408]{2,1,0:T(8,128)(2,1)}), bf16[2,128,1408]{2,1,0:T(8,128)(2,1)}, u32[]{:S(2)}, u32[]{:S(2)}) %all-to-all-start.4) | async-done | bytes 720928 | tf_op jit(solution)/shard_map/all_to_all | solution.py:24
  302.6 1.3 broadcast_in_dim.8
  303.9 4.9 %all-to-all-start = ((bf16[8,128,704]{1,2,0:T(8,128)(2,1)}), bf16[8,128,704]{1,2,0:T(8,128)(2,1)}, u32[]{:S(2)}, u32[]{:S(2)}) async-start(bf16[8,128,704]{1,2,0:T(8,128)(2,1)} %broadcast_in_dim.8), calls=%async_computation | async-start | bytes 2883584 | tf_op jit(solution)/shard_map/all_to_all | solution.py:24
  309.1 1.3 convert_reduce_fusion.2
  310.5 1.1 copy.48
  312.0 1.7 fusion.39
  314.1 12.7 %all-to-all-done = bf16[8,128,704]{1,2,0:T(8,128)(2,1)} async-done(((bf16[8,128,704]{1,2,0:T(8,128)(2,1)}), bf16[8,128,704]{1,2,0:T(8,128)(2,1)}, u32[]{:S(2)}, u32[]{:S(2)}) %all-to-all-start) | async-done | bytes 1441824 | tf_op jit(solution)/shard_map/all_to_all | solution.py:24
  326.8 10.6 %all_to_all.38 = bf16[128,8,176]{0,2,1:T(8,128)(2,1)S(1)} all-to-all(bf16[128,8,176]{0,2,1:T(8,128)(2,1)S(1)} %multiply_convert_fusion), channel_id=1, replica_groups=mesh['seq'=16,'grp'=2,'dp'=8] {'dp'}, dimensions={1} | all-to-all | bytes 720896 | tf_op jit(solution)/shard_map/all_to_all | solution.py:176
  337.4 2.7 fusion.20
  340.1 4.0 copy.49
  344.0 4.4 %multiply_add_fusion = f32[704,1408]{0,1:T(8,128)} fusion(bf16[704,1408]{0,1:T(8,128)(2,1)} %copy.49, bf16[8,704,176]{1,2,0:T(8,128)(2,1)S(1)} %all-to-all-done.1), kind=kLoop, calls=%fused_computation.7 | loop fusion | flops 4956160 | bytes 7929856 | tf_op jit(solution)/shard_map/add | solution.py:185
  348.4 5.6 %copy.50 = f32[704,1408]{1,0:T(8,128)} copy(f32[704,1408]{0,1:T(8,128)} %multiply_add_fusion) | data formatting | bytes 7929856
  354.0 33.4 %all-gather.14.cloned.1.call-done = bf16[16,704,176]{1,2,0:T(8,128)(2,1)} async-done(((bf16[1,704,176]{1,2,0:T(8,128)(2,1)}), bf16[16,704,176]{1,2,0:T(8,128)(2,1)}) %all-gather.14.cloned.1.call-update) | async-done | bytes 3964944 | tf_op jit(solution)/shard_map/all_gather | solution.py:42
  387.5 3.8 convert_reduce_fusion
  (83 shorter events, 6.6 us)
Async XLA Ops:
  7.2 167.5 %all-gather.8.cloned.1.call-start = ((), (), s32[]{:S(2)}) async-start(), calls=%async_computation.6 | async-start | bytes 7299072 | tf_op jit(solution)/shard_map/all_gather | solution.py:152
  12.1 6.0 %copy-start.16 = (s32[1,128]{1,0:T(1,128)S(1)}, s32[1,128]{1,0:T(1,128)}, u32[]{:S(2)}) copy-start(s32[1,128]{1,0:T(1,128)} %param.9) | copy-start | bytes 1540
  12.1 6.4 %copy-start = (bf16[1,128,1408]{2,1,0:T(8,128)(2,1)S(1)}, bf16[1,128,1408]{2,1,0:T(8,128)(2,1)}, u32[]{:S(2)}) copy-start(bf16[1,128,1408]{2,1,0:T(8,128)(2,1)} %param.8) | copy-start | bytes 1081348
  12.1 166.6 %all-to-all-start.3 = ((bf16[8,3,176,704]{3,2,1,0:T(8,128)(2,1)}), bf16[8,3,176,704]{3,2,1,0:T(8,128)(2,1)}, u32[]{:S(2)}, u32[]{:S(2)}) async-start(bf16[8,3,176,704]{3,2,1,0:T(8,128)(2,1)} %stack.2), calls=%async_computation.3 | async-start | bytes 12976128 | tf_op jit(solution)/shard_map/all_to_all | solution.py:107
  18.1 234.9 %all-gather.10.cloned.1.call-start = ((), (), s32[]{:S(2)}) async-start(), calls=%async_computation.7 | async-start | bytes 1531904 | tf_op jit(solution)/shard_map/all_gather | solution.py:19
  178.7 101.9 %all-gather.12.cloned.1.call-start = ((), (), s32[]{:S(2)}) async-start(), calls=%async_computation.8 | async-start | bytes 6127616 | tf_op jit(solution)/shard_map/all_gather | solution.py:19
  182.1 4.1 %copy-start.13 = (bf16[704,176]{0,1:T(8,128)(2,1)S(1)}, bf16[704,176]{0,1:T(8,128)(2,1)}, u32[]{:S(2)}) copy-start(bf16[704,176]{0,1:T(8,128)(2,1)} %param.14) | copy-start | bytes 743428
  187.7 7.6 %copy-start.14 = (f32[1408]{0:T(1024)S(1)}, f32[1408]{0:T(1024)}, u32[]{:S(2)}) copy-start(f32[1408]{0:T(1024)} %param.15) | copy-start | bytes 16900
  187.7 8.1 %copy-start.17 = (u32[256]{0:T(256)S(1)}, u32[256]{0:T(256)}, u32[]{:S(2)}) copy-start(u32[256]{0:T(256)} %constant.56) | copy-start | bytes 3076
  187.7 9.4 %copy-start.15 = (s32[1,192]{1,0:T(1,128)S(1)}, s32[1,192]{1,0:T(1,128)}, u32[]{:S(2)}) copy-start(s32[1,192]{1,0:T(1,128)} %param.10) | copy-start | bytes 2308
  187.7 73.8 %all-to-all-start.1 = ((bf16[8,704,176]{1,2,0:T(8,128)(2,1)}), bf16[8,704,176]{1,2,0:T(8,128)(2,1)S(1)}, u32[]{:S(2)}, u32[]{:S(2)}) async-start(bf16[8,704,176]{1,2,0:T(8,128)(2,1)} %broadcast_in_dim.9), calls=%async_computation.1 | async-start | bytes 4325376 | tf_op jit(solution)/shard_map/all_to_all | solution.py:24
  195.3 60.7 %copy-start.4 = (f32[128,704]{1,0:T(8,128)}, f32[128,704]{1,0:T(8,128)S(1)}, u32[]{:S(2)}) copy-start(f32[128,704]{1,0:T(8,128)S(1)} %get-tuple-element.23) | copy-start | bytes 1081348
  195.3 60.7 %copy-start.5 = (f32[128,704]{1,0:T(8,128)}, f32[128,704]{1,0:T(8,128)S(1)}, u32[]{:S(2)}) copy-start(f32[128,704]{1,0:T(8,128)S(1)} %get-tuple-element.24) | copy-start | bytes 1081348
  259.7 1.2 copy-start.11
  263.3 12.4 %all-to-all-start.2 = ((bf16[2,128,1408]{2,1,0:T(8,128)(2,1)}), bf16[2,128,1408]{2,1,0:T(8,128)(2,1)}, u32[]{:S(2)}, u32[]{:S(2)}) async-start(bf16[2,128,1408]{2,1,0:T(8,128)(2,1)} %broadcast_in_dim.10), calls=%async_computation.2 | async-start | bytes 1441792 | tf_op jit(solution)/shard_map/all_to_all | solution.py:24
  276.9 0.9 copy-start.3
  280.5 14.0 %copy-start.2 = (f32[128,1408]{1,0:T(8,128)}, f32[128,1408]{1,0:T(8,128)S(1)}, u32[]{:S(2)}) copy-start(f32[128,1408]{1,0:T(8,128)S(1)} %get-tuple-element.11) | copy-start | bytes 2162692
  280.6 3.5 copy-start.12
  287.1 1.8 copy-start.1
  290.3 12.4 %all-to-all-start.4 = ((bf16[2,128,1408]{2,1,0:T(8,128)(2,1)}), bf16[2,128,1408]{2,1,0:T(8,128)(2,1)}, u32[]{:S(2)}, u32[]{:S(2)}) async-start(bf16[2,128,1408]{2,1,0:T(8,128)(2,1)} %broadcast_in_dim.11), calls=%async_computation.4 | async-start | bytes 1441792 | tf_op jit(solution)/shard_map/all_to_all | solution.py:24
  303.9 22.9 %all-to-all-start = ((bf16[8,128,704]{1,2,0:T(8,128)(2,1)}), bf16[8,128,704]{1,2,0:T(8,128)(2,1)}, u32[]{:S(2)}, u32[]{:S(2)}) async-start(bf16[8,128,704]{1,2,0:T(8,128)(2,1)} %broadcast_in_dim.8), calls=%async_computation | async-start | bytes 2883584 | tf_op jit(solution)/shard_map/all_to_all | solution.py:24
  308.8 78.7 %all-gather.14.cloned.1.call-start = ((), (), s32[]{:S(2)}) async-start(), calls=%async_computation.9 | async-start | bytes 4595712 | tf_op jit(solution)/shard_map/all_gather | solution.py:42
  311.7 2.0 copy-start.6
  311.7 2.0 copy-start.7
  311.7 2.0 copy-start.8
  311.7 2.0 copy-start.9
  311.7 2.0 copy-start.10
Sparse Core Ops, SparseCore 0:
  9.8 164.8 all-gather.7
  178.8 45.8 all-gather.9
  226.5 53.2 all-gather.11
  340.2 47.2 all-gather.13
